TPU v7x, 256 devices: a whole 4x4x8 slice. The times are simulated.
256 devices in a mesh: section: 8 (over z_lo, core), dp: 8 (over y, z_hi), tensor: 4 (over x).
Axes of the slice: x: 4, y: 4, z: 8 (z_hi: 2, z_lo: 4; z = z_hi * 4 + z_lo), core: 2. Of those that a mesh axis runs over, the one named last changes fastest.
Arguments:
- inputs: bfloat16 [32, 2, 64, 2560], P('dp', None, None, ('section', 'tensor')), parts along dimension 0, may hold values from -18 to 18
- sequence_jobs: int32 [32, 2, 1], P('dp'), parts along dimension 0, may hold values from 0 to 3
- entry_sequence: int32 [32], P('dp'), parts along dimension 0, may hold values from 0 to 3, each once
- layer_norm_gain: float32 [8, 2560], P('section'), may hold values from 0.25 to 1.75
- frozen_query_matrix: bfloat16 [8, 2560, 2560], P('section', None, 'tensor'), may hold values from -1 to 1
- frozen_key_matrix: bfloat16 [8, 2560, 2560], P('section', None, 'tensor'), may hold values from -24 to 24
- frozen_value_matrix: bfloat16 [8, 2560, 2560], P('section', None, 'tensor'), may hold values from -0.125 to 0.125
- frozen_output_matrix: bfloat16 [8, 2560, 2560], P('section', 'tensor'), may hold values from -0.125 to 0.125
- adapter_down_maps: bfloat16 [8, 2560, 128], P('section', 'tensor'), may hold values from -0.125 to 0.125
- adapter_up_maps: bfloat16 [8, 2, 64, 2560], P('section', None, None, 'tensor'), may hold values from -1.5 to 1.5
Outputs:
- finished: bfloat16 [32, 2, 64, 2560], P('dp', None, None, ('section', 'tensor')), parts along dimension 0
There are 8 independent parts, one for each index of `dp`. A program takes and returns all parts, laid end to end along the dimension named above; an argument that names none is the same for every part. Nothing has to cross between parts.
Inputs may be any that keep to these rules, and one draw needn't show every extreme that they name: `sequence_jobs`: every one of the 4 jobs owns at least one sequence. `entry_sequence`: a permutation of the 4 micro-batches.
All inputs are finite; a program needn't handle non-finite values.
Results may differ from a plain program's by a relative error of at most 0.039.
Values may be sent and summed in bfloat16 or wider, within the bound.
A program may use at most 64 MiB of HBM per device.

v0:
```python
import jax
import jax.numpy as jnp
from jax import lax
from jax.sharding import PartitionSpec as P

HEAD_DIM = 128
ADAPTER_RANK = 16
ADAPTER_JOBS = 4


adapter_scale = 2.0


def sent_to_all(array, axis):
    peers = lax.axis_size(axis)
    return lax.all_to_all(
        jnp.broadcast_to(array[None], (peers, *array.shape)), axis, 0, 0, tiled=True
    )


def over_copies(array, axis):
    everything = sent_to_all(array, axis)
    return jnp.sum(everything, axis=0)


def taken_together(array, axis):
    everything = sent_to_all(array, axis)
    return jnp.sum(everything.astype(jnp.float32), axis=0)


def shifted(value, axis, steps):
    count = lax.axis_size(axis)
    leading, last = (max(0, -steps), min(count, count - steps))
    return lax.ppermute(value, axis, [(source, source + steps) for source in range(leading, last)])


def from_root(array, axis, root):
    return lax.dynamic_index_in_dim(lax.all_gather(array, axis), root, 0, keepdims=False)


def laid_out(blocks, dim):
    blocks = jnp.moveaxis(blocks, 0, dim)
    dims = blocks.shape
    return blocks.reshape(*dims[:dim], dims[dim] * dims[dim + 1], *dims[dim + 2 :])


def gathered_copies(array, axis, dim):
    blocks = sent_to_all(array, axis)
    return laid_out(blocks, dim)


def attend(query_rows, key_vecs, value_rows, head_groupings, sequence_length):
    head_count = query_rows.shape[1] // HEAD_DIM
    grid_shape = (head_groupings, sequence_length, head_count, HEAD_DIM)
    scores = jnp.einsum(
        "bqhd,bkhd->bhqk",
        query_rows.reshape(grid_shape),
        key_vecs.reshape(grid_shape),
        preferred_element_type=jnp.float32,
    ) * HEAD_DIM ** (-0.5)
    causal = lax.broadcasted_iota(
        jnp.int32, (sequence_length, sequence_length), 0
    ) >= lax.broadcasted_iota(jnp.int32, (sequence_length, sequence_length), 1)
    scores = jnp.where(causal, scores, -jnp.inf)
    row_max = jnp.max(scores, axis=-1, keepdims=True)
    weights = jnp.exp(scores - row_max)
    probabilities = (weights / jnp.sum(weights, axis=-1, keepdims=True)).astype(jnp.bfloat16)
    mixture = jnp.einsum(
        "bhqk,bkhd->bqhd",
        probabilities,
        value_rows.reshape(grid_shape),
        preferred_element_type=jnp.float32,
    )
    return mixture.astype(jnp.bfloat16).reshape(
        head_groupings * sequence_length, head_count * HEAD_DIM
    )


def prepare_inputs(
    complete_result, inverse_norm_scale, adapter_rows, partition_number, column_slice
):
    widened = complete_result.astype(jnp.float32)
    meansq = jnp.mean(widened * widened, axis=-1, keepdims=True)
    normalized_input = (widened * lax.rsqrt(meansq + 1e-05) * inverse_norm_scale).astype(
        jnp.bfloat16
    )
    local_normalized = lax.dynamic_slice_in_dim(
        normalized_input, partition_number * column_slice, column_slice, 1
    )
    return (
        normalized_input,
        jnp.dot(local_normalized, adapter_rows, preferred_element_type=jnp.float32),
    )


def final_output(
    normalized_input,
    lowrank_products,
    query_matrix,
    key_matrix,
    value_matrix,
    output_matrix,
    adapter_upper_part,
    head_groupings,
    sequence_length,
):
    middle_result = lowrank_products.shape[1] // 2
    query_rows = (
        jnp.dot(normalized_input, query_matrix, preferred_element_type=jnp.float32)
        + adapter_scale
        * jnp.dot(
            lowrank_products[:, :middle_result],
            adapter_upper_part[0],
            preferred_element_type=jnp.float32,
        )
    ).astype(jnp.bfloat16)
    key_vecs = jnp.dot(normalized_input, key_matrix, preferred_element_type=jnp.float32).astype(
        jnp.bfloat16
    )
    value_rows = (
        jnp.dot(normalized_input, value_matrix, preferred_element_type=jnp.float32)
        + adapter_scale
        * jnp.dot(
            lowrank_products[:, middle_result:],
            adapter_upper_part[1],
            preferred_element_type=jnp.float32,
        )
    ).astype(jnp.bfloat16)
    heads = attend(query_rows, key_vecs, value_rows, head_groupings, sequence_length)
    return (
        jnp.dot(heads, output_matrix, preferred_element_type=jnp.float32)
        .astype(jnp.bfloat16)
        .astype(jnp.float32)
    )


def shards(
    inputs,
    sequence_jobs,
    entry_sequence,
    layer_norm_gain,
    frozen_query_matrix,
    frozen_key_matrix,
    frozen_value_matrix,
    frozen_output_matrix,
    adapter_down_maps,
    adapter_up_maps,
):
    sections = lax.axis_size("section")
    across = lax.axis_size("tensor")
    section_id = lax.axis_index("section")
    partition_number = lax.axis_index("tensor")
    entire = lax.all_gather(inputs, ("section", "tensor"), axis=3, tiled=True)
    batches, head_groupings, sequence_length, features = entire.shape
    column_slice = frozen_query_matrix.shape[2]
    lowrank_width = adapter_down_maps.shape[2]
    tok_rows = head_groupings * sequence_length
    step_count = batches + sections - 1

    def compute(complete_result, step_idx):
        position = step_idx - section_id
        active = jnp.logical_and(position >= 0, position < batches)
        chosen = entry_sequence[jnp.clip(position, 0, batches - 1)]
        seq_jobs = lax.dynamic_index_in_dim(sequence_jobs, chosen, 0, keepdims=False)
        job_per_row = jnp.repeat(seq_jobs[:, 0], sequence_length)
        normalized_input, part_codes = lax.cond(
            active,
            lambda: prepare_inputs(
                complete_result,
                layer_norm_gain[0],
                adapter_down_maps[0],
                partition_number,
                column_slice,
            ),
            lambda: (
                jnp.zeros((tok_rows, features), jnp.bfloat16),
                jnp.zeros((tok_rows, lowrank_width), jnp.float32),
            ),
        )
        summed_codes = over_copies(part_codes, "tensor")
        column_job = (
            lax.broadcasted_iota(jnp.int32, (lowrank_width,), 0) // ADAPTER_RANK % ADAPTER_JOBS
        )
        lowrank_products = jnp.where(
            column_job[None, :] == job_per_row[:, None], summed_codes, 0.0
        ).astype(jnp.bfloat16)
        return lax.cond(
            active,
            lambda: final_output(
                normalized_input,
                lowrank_products,
                frozen_query_matrix[0],
                frozen_key_matrix[0],
                frozen_value_matrix[0],
                frozen_output_matrix[0],
                adapter_up_maps[0],
                head_groupings,
                sequence_length,
            ),
            lambda: jnp.zeros((tok_rows, features), jnp.float32),
        )

    def injected(step_idx):
        chosen = entry_sequence[jnp.minimum(step_idx, batches - 1)]
        return lax.dynamic_index_in_dim(entire, chosen, 0, keepdims=False).reshape(
            tok_rows, features
        )

    def record(stored, step_idx, piece):
        out_slot = step_idx - (sections - 1)
        keeping = jnp.logical_and(section_id == sections - 1, out_slot >= 0)
        updated = lax.dynamic_update_index_in_dim(stored, piece, jnp.maximum(out_slot, 0), 0)
        return jnp.where(keeping, updated, stored)

    stored = jnp.zeros((batches, tok_rows, column_slice), jnp.bfloat16)

    def advance(step_idx, carried):
        arrived, stored = carried
        complete_result = jnp.where(section_id == 0, injected(step_idx), arrived)
        term = compute(complete_result, step_idx)
        summed = taken_together(term.astype(jnp.bfloat16), "tensor").astype(jnp.float32)
        updated_x = (complete_result.astype(jnp.float32) + summed).astype(jnp.bfloat16)
        own_cols = lax.dynamic_slice_in_dim(
            updated_x, partition_number * column_slice, column_slice, 1
        )
        stored = record(stored, step_idx, own_cols)
        arrived = shifted(updated_x, ("section", "tensor"), across)
        return (arrived, stored)

    initial = jnp.zeros((tok_rows, features), jnp.bfloat16)
    arrived, stored = lax.fori_loop(0, step_count, advance, (initial, stored))
    result = from_root(stored, "section", sections - 1)
    complete = gathered_copies(result, "tensor", 2)
    width = features // (sections * across)
    piece = lax.dynamic_slice_in_dim(
        complete, (section_id * across + partition_number) * width, width, 2
    )
    return piece.reshape(batches, head_groupings, sequence_length, width)


def solution(mesh):
    in_specs = (
        P("dp", None, None, ("section", "tensor")),
        P("dp", None, None),
        P("dp"),
        P("section", None),
        P("section", None, "tensor"),
        P("section", None, "tensor"),
        P("section", None, "tensor"),
        P("section", "tensor", None),
        P("section", "tensor", None),
        P("section", None, None, "tensor"),
    )
    out_specs = P("dp", None, None, ("section", "tensor"))
    return jax.shard_map(shards, mesh=mesh, in_specs=in_specs, out_specs=out_specs, check_vma=False)
```

profile of v0, /device:TPU:1, one launch (start us, length us, event | category | flops | bytes accessed | tf_op | source)
XLA Modules:
  0.0 942.1 jit_solution(13096310259569025942)
XLA Ops:
  9.1 94.1 %all-gather.4.cloned.1.call-done = bf16[4,2,64,2560]{2,0,1,3:T(4,128)(2,1)} async-done(((bf16[4,2,64,80]{2,0,1,3:T(4,128)(2,1)}), bf16[4,2,64,2560]{2,0,1,3:T(4,128)(2,1)}) %all-gather.4.cloned.1.call-update) | async-done | bytes 2621456 | tf_op jit(solution)/shard_map/all_gather | solution.py:153
  103.1 8.4 copy.55
  111.7 716.4 %while.17 = (s32[]{:T(128)}, bf16[128,2560]{1,0:T(8,128)(2,1)S(1)}, bf16[4,128,640]{2,1,0:T(8,128)(2,1)S(1)}, pred[]{:T(512)}, s32[4]{0:T(128)S(1)}, /*index=5*/...) while((s32[]{:T(128)}, bf16[128,2560]{1,0:T(8,128)(2,1)S(1)}, ...), condition=%wide.region_10.11_spmd, body=%wide.region_0.10_spmd.sunk | while | flops 1747975296 | bytes 45728476 | solution.py:231
  117.2 3.7 all-to-all-start
  123.0 3.4 all-to-all-done
  126.8 20.7 %all_to_all.31 = bf16[4,128,2560]{2,1,0:T(8,128)(2,1)S(1)} all-to-all(bf16[4,128,2560]{2,1,0:T(8,128)(2,1)S(1)} %broadcast_in_dim.108), channel_id=1, replica_groups=mesh['section'=8,'dp'=8,'tensor'=4] {'tensor'}, dimensions={0} | all-to-all | bytes 5242880 | tf_op jit(solution)/shard_map/while/body/eval_jaxpr/all_to_all | solution.py:16
  148.0 18.5 %collective-permute-start = (bf16[128,2560]{1,0:T(8,128)(2,1)S(1)}, bf16[128,2560]{1,0:T(8,128)(2,1)S(1)}, u32[]{:S(2)}, u32[]{:S(2)}) collective-permute-start(bf16[128,2560]{1,0:T(8,128)(2,1)S(1)} %add_convert_fusion.2), channel_id=1, source_target_pairs={{0,32},{1,33},{2,34},{3,35},{32,64},{33,65},{34,66},{35,67},{64,96... | collective-permute-start | bytes 1966088 | tf_op jit(solution)/shard_map/while/body/eval_jaxpr/ppermute | solution.py:34
  166.6 7.4 collective-permute-done
  190.0 12.9 %conditional.5 = (bf16[128,2560]{1,0:T(8,128)(2,1)S(1)}) conditional(s32[]{:T(128)} %convert_element_type.123, () %tuple.63, (bf16[1,2560,640]{2,1,0:T(8,128)(2,1)}, bf16[128,2560]{1,0:T(8,128)(2,1)}, bf16[128,128]{1,0:T(8,128)(2,1)S(1)}, bf16[1,2,64,640]{3,2,1,0:T(8,128)(2,1)S(1)}, bf16[1,2560,640]{2,1,0:T(8,128)(2,1)}, ...), branch_computations={%region_5.5_spmd, %region_6.8_spmd} | conditional | flops 1720939136 | bytes 20395016 | solution.py:187
  203.1 30.3 %all_to_all.31 = bf16[4,128,2560]{2,1,0:T(8,128)(2,1)S(1)} all-to-all(bf16[4,128,2560]{2,1,0:T(8,128)(2,1)S(1)} %broadcast_in_dim.108), channel_id=1, replica_groups=mesh['section'=8,'dp'=8,'tensor'=4] {'tensor'}, dimensions={0} | all-to-all | bytes 5242880 | tf_op jit(solution)/shard_map/while/body/eval_jaxpr/all_to_all | solution.py:16
  235.9 7.4 collective-permute-done
  259.3 12.9 %conditional.5 = (bf16[128,2560]{1,0:T(8,128)(2,1)S(1)}) conditional(s32[]{:T(128)} %convert_element_type.123, () %tuple.63, (bf16[1,2560,640]{2,1,0:T(8,128)(2,1)}, bf16[128,2560]{1,0:T(8,128)(2,1)}, bf16[128,128]{1,0:T(8,128)(2,1)S(1)}, bf16[1,2,64,640]{3,2,1,0:T(8,128)(2,1)S(1)}, bf16[1,2560,640]{2,1,0:T(8,128)(2,1)}, ...), branch_computations={%region_5.5_spmd, %region_6.8_spmd} | conditional | flops 1720939136 | bytes 20395016 | solution.py:187
  272.4 31.0 %all_to_all.31 = bf16[4,128,2560]{2,1,0:T(8,128)(2,1)S(1)} all-to-all(bf16[4,128,2560]{2,1,0:T(8,128)(2,1)S(1)} %broadcast_in_dim.108), channel_id=1, replica_groups=mesh['section'=8,'dp'=8,'tensor'=4] {'tensor'}, dimensions={0} | all-to-all | bytes 5242880 | tf_op jit(solution)/shard_map/while/body/eval_jaxpr/all_to_all | solution.py:16
  306.0 7.4 collective-permute-done
  329.4 12.9 %conditional.5 = (bf16[128,2560]{1,0:T(8,128)(2,1)S(1)}) conditional(s32[]{:T(128)} %convert_element_type.123, () %tuple.63, (bf16[1,2560,640]{2,1,0:T(8,128)(2,1)}, bf16[128,2560]{1,0:T(8,128)(2,1)}, bf16[128,128]{1,0:T(8,128)(2,1)S(1)}, bf16[1,2,64,640]{3,2,1,0:T(8,128)(2,1)S(1)}, bf16[1,2560,640]{2,1,0:T(8,128)(2,1)}, ...), branch_computations={%region_5.5_spmd, %region_6.8_spmd} | conditional | flops 1720939136 | bytes 20395016 | solution.py:187
  342.5 31.0 %all_to_all.31 = bf16[4,128,2560]{2,1,0:T(8,128)(2,1)S(1)} all-to-all(bf16[4,128,2560]{2,1,0:T(8,128)(2,1)S(1)} %broadcast_in_dim.108), channel_id=1, replica_groups=mesh['section'=8,'dp'=8,'tensor'=4] {'tensor'}, dimensions={0} | all-to-all | bytes 5242880 | tf_op jit(solution)/shard_map/while/body/eval_jaxpr/all_to_all | solution.py:16
  376.0 7.4 collective-permute-done
  399.4 12.9 %conditional.5 = (bf16[128,2560]{1,0:T(8,128)(2,1)S(1)}) conditional(s32[]{:T(128)} %convert_element_type.123, () %tuple.63, (bf16[1,2560,640]{2,1,0:T(8,128)(2,1)}, bf16[128,2560]{1,0:T(8,128)(2,1)}, bf16[128,128]{1,0:T(8,128)(2,1)S(1)}, bf16[1,2,64,640]{3,2,1,0:T(8,128)(2,1)S(1)}, bf16[1,2560,640]{2,1,0:T(8,128)(2,1)}, ...), branch_computations={%region_5.5_spmd, %region_6.8_spmd} | conditional | flops 1720939136 | bytes 20395016 | solution.py:187
  412.5 20.7 %all_to_all.31 = bf16[4,128,2560]{2,1,0:T(8,128)(2,1)S(1)} all-to-all(bf16[4,128,2560]{2,1,0:T(8,128)(2,1)S(1)} %broadcast_in_dim.108), channel_id=1, replica_groups=mesh['section'=8,'dp'=8,'tensor'=4] {'tensor'}, dimensions={0} | all-to-all | bytes 5242880 | tf_op jit(solution)/shard_map/while/body/eval_jaxpr/all_to_all | solution.py:16
  433.7 6.7 collective-permute-start
  440.5 7.4 collective-permute-done
  458.8 5.0 all-to-all-done
  464.2 26.1 %all_to_all.31 = bf16[4,128,2560]{2,1,0:T(8,128)(2,1)S(1)} all-to-all(bf16[4,128,2560]{2,1,0:T(8,128)(2,1)S(1)} %broadcast_in_dim.108), channel_id=1, replica_groups=mesh['section'=8,'dp'=8,'tensor'=4] {'tensor'}, dimensions={0} | all-to-all | bytes 5242880 | tf_op jit(solution)/shard_map/while/body/eval_jaxpr/all_to_all | solution.py:16
  490.8 18.1 %collective-permute-start = (bf16[128,2560]{1,0:T(8,128)(2,1)S(1)}, bf16[128,2560]{1,0:T(8,128)(2,1)S(1)}, u32[]{:S(2)}, u32[]{:S(2)}) collective-permute-start(bf16[128,2560]{1,0:T(8,128)(2,1)S(1)} %add_convert_fusion.2), channel_id=1, source_target_pairs={{0,32},{1,33},{2,34},{3,35},{32,64},{33,65},{34,66},{35,67},{64,96... | collective-permute-start | bytes 1966088 | tf_op jit(solution)/shard_map/while/body/eval_jaxpr/ppermute | solution.py:34
  509.0 7.4 collective-permute-done
  527.3 4.8 all-to-all-done
  532.5 20.7 %all_to_all.31 = bf16[4,128,2560]{2,1,0:T(8,128)(2,1)S(1)} all-to-all(bf16[4,128,2560]{2,1,0:T(8,128)(2,1)S(1)} %broadcast_in_dim.108), channel_id=1, replica_groups=mesh['section'=8,'dp'=8,'tensor'=4] {'tensor'}, dimensions={0} | all-to-all | bytes 5242880 | tf_op jit(solution)/shard_map/while/body/eval_jaxpr/all_to_all | solution.py:16
  553.7 15.0 %collective-permute-start = (bf16[128,2560]{1,0:T(8,128)(2,1)S(1)}, bf16[128,2560]{1,0:T(8,128)(2,1)S(1)}, u32[]{:S(2)}, u32[]{:S(2)}) collective-permute-start(bf16[128,2560]{1,0:T(8,128)(2,1)S(1)} %add_convert_fusion.2), channel_id=1, source_target_pairs={{0,32},{1,33},{2,34},{3,35},{32,64},{33,65},{34,66},{35,67},{64,96... | collective-permute-start | bytes 1966088 | tf_op jit(solution)/shard_map/while/body/eval_jaxpr/ppermute | solution.py:34
  568.8 7.4 collective-permute-done
  587.1 5.1 all-to-all-done
  592.6 20.7 %all_to_all.31 = bf16[4,128,2560]{2,1,0:T(8,128)(2,1)S(1)} all-to-all(bf16[4,128,2560]{2,1,0:T(8,128)(2,1)S(1)} %broadcast_in_dim.108), channel_id=1, replica_groups=mesh['section'=8,'dp'=8,'tensor'=4] {'tensor'}, dimensions={0} | all-to-all | bytes 5242880 | tf_op jit(solution)/shard_map/while/body/eval_jaxpr/all_to_all | solution.py:16
  613.8 19.3 %collective-permute-start = (bf16[128,2560]{1,0:T(8,128)(2,1)S(1)}, bf16[128,2560]{1,0:T(8,128)(2,1)S(1)}, u32[]{:S(2)}, u32[]{:S(2)}) collective-permute-start(bf16[128,2560]{1,0:T(8,128)(2,1)S(1)} %add_convert_fusion.2), channel_id=1, source_target_pairs={{0,32},{1,33},{2,34},{3,35},{32,64},{33,65},{34,66},{35,67},{64,96... | collective-permute-start | bytes 1966088 | tf_op jit(solution)/shard_map/while/body/eval_jaxpr/ppermute | solution.py:34
  633.2 7.4 collective-permute-done
  651.5 5.1 all-to-all-done
  657.0 20.7 %all_to_all.31 = bf16[4,128,2560]{2,1,0:T(8,128)(2,1)S(1)} all-to-all(bf16[4,128,2560]{2,1,0:T(8,128)(2,1)S(1)} %broadcast_in_dim.108), channel_id=1, replica_groups=mesh['section'=8,'dp'=8,'tensor'=4] {'tensor'}, dimensions={0} | all-to-all | bytes 5242880 | tf_op jit(solution)/shard_map/while/body/eval_jaxpr/all_to_all | solution.py:16
  678.2 19.3 %collective-permute-start = (bf16[128,2560]{1,0:T(8,128)(2,1)S(1)}, bf16[128,2560]{1,0:T(8,128)(2,1)S(1)}, u32[]{:S(2)}, u32[]{:S(2)}) collective-permute-start(bf16[128,2560]{1,0:T(8,128)(2,1)S(1)} %add_convert_fusion.2), channel_id=1, source_target_pairs={{0,32},{1,33},{2,34},{3,35},{32,64},{33,65},{34,66},{35,67},{64,96... | collective-permute-start | bytes 1966088 | tf_op jit(solution)/shard_map/while/body/eval_jaxpr/ppermute | solution.py:34
  697.6 7.4 collective-permute-done
  715.9 5.0 all-to-all-done
  721.4 20.7 %all_to_all.31 = bf16[4,128,2560]{2,1,0:T(8,128)(2,1)S(1)} all-to-all(bf16[4,128,2560]{2,1,0:T(8,128)(2,1)S(1)} %broadcast_in_dim.108), channel_id=1, replica_groups=mesh['section'=8,'dp'=8,'tensor'=4] {'tensor'}, dimensions={0} | all-to-all | bytes 5242880 | tf_op jit(solution)/shard_map/while/body/eval_jaxpr/all_to_all | solution.py:16
  742.5 14.2 %collective-permute-start = (bf16[128,2560]{1,0:T(8,128)(2,1)S(1)}, bf16[128,2560]{1,0:T(8,128)(2,1)S(1)}, u32[]{:S(2)}, u32[]{:S(2)}) collective-permute-start(bf16[128,2560]{1,0:T(8,128)(2,1)S(1)} %add_convert_fusion.2), channel_id=1, source_target_pairs={{0,32},{1,33},{2,34},{3,35},{32,64},{33,65},{34,66},{35,67},{64,96... | collective-permute-start | bytes 1966088 | tf_op jit(solution)/shard_map/while/body/eval_jaxpr/ppermute | solution.py:34
  756.8 7.4 collective-permute-done
  775.1 5.1 all-to-all-done
  780.6 20.7 %all_to_all.31 = bf16[4,128,2560]{2,1,0:T(8,128)(2,1)S(1)} all-to-all(bf16[4,128,2560]{2,1,0:T(8,128)(2,1)S(1)} %broadcast_in_dim.108), channel_id=1, replica_groups=mesh['section'=8,'dp'=8,'tensor'=4] {'tensor'}, dimensions={0} | all-to-all | bytes 5242880 | tf_op jit(solution)/shard_map/while/body/eval_jaxpr/all_to_all | solution.py:16
  801.8 18.8 %collective-permute-start = (bf16[128,2560]{1,0:T(8,128)(2,1)S(1)}, bf16[128,2560]{1,0:T(8,128)(2,1)S(1)}, u32[]{:S(2)}, u32[]{:S(2)}) collective-permute-start(bf16[128,2560]{1,0:T(8,128)(2,1)S(1)} %add_convert_fusion.2), channel_id=1, source_target_pairs={{0,32},{1,33},{2,34},{3,35},{32,64},{33,65},{34,66},{35,67},{64,96... | collective-permute-start | bytes 1966088 | tf_op jit(solution)/shard_map/while/body/eval_jaxpr/ppermute | solution.py:34
  820.7 7.4 collective-permute-done
  829.0 66.0 %all-gather.6.cloned.1.call-done = bf16[32,128,640]{2,1,0:T(8,128)(2,1)} async-done(((bf16[4,128,640]{2,1,0:T(8,128)(2,1)}), bf16[32,128,640]{2,1,0:T(8,128)(2,1)}) %all-gather.6.cloned.1.call-update) | async-done | bytes 5242896 | tf_op jit(solution)/shard_map/all_gather | solution.py:38
  898.0 4.0 all-to-all-start.2
  902.0 29.0 %all-to-all-done.2 = bf16[4,4,128,640]{3,2,1,0:T(8,128)(2,1)S(1)} async-done(((bf16[4,4,128,640]{3,2,1,0:T(8,128)(2,1)}), bf16[4,4,128,640]{3,2,1,0:T(8,128)(2,1)S(1)}, u32[]{:S(2)}, u32[]{:S(2)}) %all-to-all-start.2) | async-done | bytes 2621472 | tf_op jit(solution)/shard_map/all_to_all | solution.py:16
  (309 shorter events, 188.0 us)
Async XLA Ops:
  6.5 96.6 %all-gather.4.cloned.1.call-start = ((), (), s32[]{:S(2)}) async-start(), calls=%async_computation.3 | async-start | bytes 5406720 | tf_op jit(solution)/shard_map/all_gather | solution.py:153
  8.3 886.8 %all-gather.6.cloned.1.call-start = ((), (), s32[]{:S(2)}) async-start(), calls=%async_computation.4 | async-start | bytes 5898240 | tf_op jit(solution)/shard_map/all_gather | solution.py:38
  9.1 102.6 %copy-start.1 = (bf16[1,2,64,640]{3,2,1,0:T(8,128)(2,1)S(1)}, bf16[1,2,64,640]{3,2,1,0:T(8,128)(2,1)}, u32[]{:S(2)}) copy-start(bf16[1,2,64,640]{3,2,1,0:T(8,128)(2,1)} %param.25) | copy-start | bytes 491524
  9.1 102.6 %copy-start.2 = (bf16[1,640,128]{2,1,0:T(8,128)(2,1)S(1)}, bf16[1,640,128]{2,1,0:T(8,128)(2,1)}, u32[]{:S(2)}) copy-start(bf16[1,640,128]{2,1,0:T(8,128)(2,1)} %param.24) | copy-start | bytes 491524
  9.1 102.6 %copy-start.3 = (f32[1,2560]{1,0:T(1,128)S(1)}, f32[1,2560]{1,0:T(1,128)}, u32[]{:S(2)}) copy-start(f32[1,2560]{1,0:T(1,128)} %param.19) | copy-start | bytes 30724
  9.1 102.6 %copy-start.4 = (s32[4]{0:T(128)S(1)}, s32[4]{0:T(128)}, u32[]{:S(2)}) copy-start(s32[4]{0:T(128)} %param.18) | copy-start | bytes 52
  117.2 9.2 all-to-all-start
  148.0 26.1 %collective-permute-start = (bf16[128,2560]{1,0:T(8,128)(2,1)S(1)}, bf16[128,2560]{1,0:T(8,128)(2,1)S(1)}, u32[]{:S(2)}, u32[]{:S(2)}) collective-permute-start(bf16[128,2560]{1,0:T(8,128)(2,1)S(1)} %add_convert_fusion.2), channel_id=1, source_target_pairs={{0,32},{1,33},{2,34},{3,35},{32,64},{33,65},{34,66},{35,67},{64,96... | collective-permute-start | bytes 1966088 | tf_op jit(solution)/shard_map/while/body/eval_jaxpr/ppermute | solution.py:34
  181.0 8.9 all-to-all-start
  233.9 9.4 %collective-permute-start = (bf16[128,2560]{1,0:T(8,128)(2,1)S(1)}, bf16[128,2560]{1,0:T(8,128)(2,1)S(1)}, u32[]{:S(2)}, u32[]{:S(2)}) collective-permute-start(bf16[128,2560]{1,0:T(8,128)(2,1)S(1)} %add_convert_fusion.2), channel_id=1, source_target_pairs={{0,32},{1,33},{2,34},{3,35},{32,64},{33,65},{34,66},{35,67},{64,96... | collective-permute-start | bytes 1966088 | tf_op jit(solution)/shard_map/while/body/eval_jaxpr/ppermute | solution.py:34
  250.3 8.9 all-to-all-start
  304.0 9.4 %collective-permute-start = (bf16[128,2560]{1,0:T(8,128)(2,1)S(1)}, bf16[128,2560]{1,0:T(8,128)(2,1)S(1)}, u32[]{:S(2)}, u32[]{:S(2)}) collective-permute-start(bf16[128,2560]{1,0:T(8,128)(2,1)S(1)} %add_convert_fusion.2), channel_id=1, source_target_pairs={{0,32},{1,33},{2,34},{3,35},{32,64},{33,65},{34,66},{35,67},{64,96... | collective-permute-start | bytes 1966088 | tf_op jit(solution)/shard_map/while/body/eval_jaxpr/ppermute | solution.py:34
  320.4 8.9 all-to-all-start
  374.0 9.4 %collective-permute-start = (bf16[128,2560]{1,0:T(8,128)(2,1)S(1)}, bf16[128,2560]{1,0:T(8,128)(2,1)S(1)}, u32[]{:S(2)}, u32[]{:S(2)}) collective-permute-start(bf16[128,2560]{1,0:T(8,128)(2,1)S(1)} %add_convert_fusion.2), channel_id=1, source_target_pairs={{0,32},{1,33},{2,34},{3,35},{32,64},{33,65},{34,66},{35,67},{64,96... | collective-permute-start | bytes 1966088 | tf_op jit(solution)/shard_map/while/body/eval_jaxpr/ppermute | solution.py:34
  390.4 8.9 all-to-all-start
  433.7 14.2 %collective-permute-start = (bf16[128,2560]{1,0:T(8,128)(2,1)S(1)}, bf16[128,2560]{1,0:T(8,128)(2,1)S(1)}, u32[]{:S(2)}, u32[]{:S(2)}) collective-permute-start(bf16[128,2560]{1,0:T(8,128)(2,1)S(1)} %add_convert_fusion.2), channel_id=1, source_target_pairs={{0,32},{1,33},{2,34},{3,35},{32,64},{33,65},{34,66},{35,67},{64,96... | collective-permute-start | bytes 1966088 | tf_op jit(solution)/shard_map/while/body/eval_jaxpr/ppermute | solution.py:34
  453.3 10.5 %all-to-all-start = ((f32[4,128,128]{2,1,0:T(8,128)}), f32[4,128,128]{2,1,0:T(8,128)S(1)}, u32[]{:S(2)}, u32[]{:S(2)}) async-start(f32[4,128,128]{2,1,0:T(8,128)} %broadcast_in_dim.106), calls=%async_computation | async-start | bytes 524288 | tf_op jit(solution)/shard_map/while/body/eval_jaxpr/all_to_all | solution.py:16
  490.8 25.6 %collective-permute-start = (bf16[128,2560]{1,0:T(8,128)(2,1)S(1)}, bf16[128,2560]{1,0:T(8,128)(2,1)S(1)}, u32[]{:S(2)}, u32[]{:S(2)}) collective-permute-start(bf16[128,2560]{1,0:T(8,128)(2,1)S(1)} %add_convert_fusion.2), channel_id=1, source_target_pairs={{0,32},{1,33},{2,34},{3,35},{32,64},{33,65},{34,66},{35,67},{64,96... | collective-permute-start | bytes 1966088 | tf_op jit(solution)/shard_map/while/body/eval_jaxpr/ppermute | solution.py:34
  521.8 10.3 %all-to-all-start = ((f32[4,128,128]{2,1,0:T(8,128)}), f32[4,128,128]{2,1,0:T(8,128)S(1)}, u32[]{:S(2)}, u32[]{:S(2)}) async-start(f32[4,128,128]{2,1,0:T(8,128)} %broadcast_in_dim.106), calls=%async_computation | async-start | bytes 524288 | tf_op jit(solution)/shard_map/while/body/eval_jaxpr/all_to_all | solution.py:16
  553.7 22.5 %collective-permute-start = (bf16[128,2560]{1,0:T(8,128)(2,1)S(1)}, bf16[128,2560]{1,0:T(8,128)(2,1)S(1)}, u32[]{:S(2)}, u32[]{:S(2)}) collective-permute-start(bf16[128,2560]{1,0:T(8,128)(2,1)S(1)} %add_convert_fusion.2), channel_id=1, source_target_pairs={{0,32},{1,33},{2,34},{3,35},{32,64},{33,65},{34,66},{35,67},{64,96... | collective-permute-start | bytes 1966088 | tf_op jit(solution)/shard_map/while/body/eval_jaxpr/ppermute | solution.py:34
  581.6 10.6 %all-to-all-start = ((f32[4,128,128]{2,1,0:T(8,128)}), f32[4,128,128]{2,1,0:T(8,128)S(1)}, u32[]{:S(2)}, u32[]{:S(2)}) async-start(f32[4,128,128]{2,1,0:T(8,128)} %broadcast_in_dim.106), calls=%async_computation | async-start | bytes 524288 | tf_op jit(solution)/shard_map/while/body/eval_jaxpr/all_to_all | solution.py:16
  613.8 26.8 %collective-permute-start = (bf16[128,2560]{1,0:T(8,128)(2,1)S(1)}, bf16[128,2560]{1,0:T(8,128)(2,1)S(1)}, u32[]{:S(2)}, u32[]{:S(2)}) collective-permute-start(bf16[128,2560]{1,0:T(8,128)(2,1)S(1)} %add_convert_fusion.2), channel_id=1, source_target_pairs={{0,32},{1,33},{2,34},{3,35},{32,64},{33,65},{34,66},{35,67},{64,96... | collective-permute-start | bytes 1966088 | tf_op jit(solution)/shard_map/while/body/eval_jaxpr/ppermute | solution.py:34
  646.0 10.6 %all-to-all-start = ((f32[4,128,128]{2,1,0:T(8,128)}), f32[4,128,128]{2,1,0:T(8,128)S(1)}, u32[]{:S(2)}, u32[]{:S(2)}) async-start(f32[4,128,128]{2,1,0:T(8,128)} %broadcast_in_dim.106), calls=%async_computation | async-start | bytes 524288 | tf_op jit(solution)/shard_map/while/body/eval_jaxpr/all_to_all | solution.py:16
  678.2 26.8 %collective-permute-start = (bf16[128,2560]{1,0:T(8,128)(2,1)S(1)}, bf16[128,2560]{1,0:T(8,128)(2,1)S(1)}, u32[]{:S(2)}, u32[]{:S(2)}) collective-permute-start(bf16[128,2560]{1,0:T(8,128)(2,1)S(1)} %add_convert_fusion.2), channel_id=1, source_target_pairs={{0,32},{1,33},{2,34},{3,35},{32,64},{33,65},{34,66},{35,67},{64,96... | collective-permute-start | bytes 1966088 | tf_op jit(solution)/shard_map/while/body/eval_jaxpr/ppermute | solution.py:34
  710.4 10.5 %all-to-all-start = ((f32[4,128,128]{2,1,0:T(8,128)}), f32[4,128,128]{2,1,0:T(8,128)S(1)}, u32[]{:S(2)}, u32[]{:S(2)}) async-start(f32[4,128,128]{2,1,0:T(8,128)} %broadcast_in_dim.106), calls=%async_computation | async-start | bytes 524288 | tf_op jit(solution)/shard_map/while/body/eval_jaxpr/all_to_all | solution.py:16
  742.5 21.7 %collective-permute-start = (bf16[128,2560]{1,0:T(8,128)(2,1)S(1)}, bf16[128,2560]{1,0:T(8,128)(2,1)S(1)}, u32[]{:S(2)}, u32[]{:S(2)}) collective-permute-start(bf16[128,2560]{1,0:T(8,128)(2,1)S(1)} %add_convert_fusion.2), channel_id=1, source_target_pairs={{0,32},{1,33},{2,34},{3,35},{32,64},{33,65},{34,66},{35,67},{64,96... | collective-permute-start | bytes 1966088 | tf_op jit(solution)/shard_map/while/body/eval_jaxpr/ppermute | solution.py:34
  769.6 10.6 %all-to-all-start = ((f32[4,128,128]{2,1,0:T(8,128)}), f32[4,128,128]{2,1,0:T(8,128)S(1)}, u32[]{:S(2)}, u32[]{:S(2)}) async-start(f32[4,128,128]{2,1,0:T(8,128)} %broadcast_in_dim.106), calls=%async_computation | async-start | bytes 524288 | tf_op jit(solution)/shard_map/while/body/eval_jaxpr/all_to_all | solution.py:16
  801.8 26.3 %collective-permute-start = (bf16[128,2560]{1,0:T(8,128)(2,1)S(1)}, bf16[128,2560]{1,0:T(8,128)(2,1)S(1)}, u32[]{:S(2)}, u32[]{:S(2)}) collective-permute-start(bf16[128,2560]{1,0:T(8,128)(2,1)S(1)} %add_convert_fusion.2), channel_id=1, source_target_pairs={{0,32},{1,33},{2,34},{3,35},{32,64},{33,65},{34,66},{35,67},{64,96... | collective-permute-start | bytes 1966088 | tf_op jit(solution)/shard_map/while/body/eval_jaxpr/ppermute | solution.py:34
  828.2 0.9 copy-start
  898.0 33.0 %all-to-all-start.2 = ((bf16[4,4,128,640]{3,2,1,0:T(8,128)(2,1)}), bf16[4,4,128,640]{3,2,1,0:T(8,128)(2,1)S(1)}, u32[]{:S(2)}, u32[]{:S(2)}) async-start(bf16[4,4,128,640]{3,2,1,0:T(8,128)(2,1)} %broadcast_in_dim.97), calls=%async_computation.2 | async-start | bytes 5242880 | tf_op jit(solution)/shard_map/all_to_all | solution.py:16
Sparse Core Ops, SparseCore 0:
  9.1 93.9 all-gather.3
  829.2 65.8 all-gather.5
where the time goes:
time: 948 us; the launch traced here: 942 us
  waiting for transfers between devices  318 us (34%)
  blocking collectives  263 us (28%)
  starting transfers between devices  177 us (19%)
  local copies, waits for them, and re-layouts  59.7 us (6%)
  matrix products  52.2 us (6%)
  loops' own time  43.9 us (5%)
  other arithmetic  14.4 us (2%)
  between operations  13.5 us (1%)
    all_to_all x11, blocking collectives, sent_to_all(): lax.all_to_all(jnp.broadcast_to(array[None], (peers, *array.shape)), axis...  263 us
    ppermute x11, starting transfers between devices, shifted(): lax.ppermute(value, axis, [(source, source + steps) for source in range(l...  136 us
    all_gather x1, waiting for transfers between devices, shards(): entire = lax.all_gather(inputs, ('section', 'tensor'), axis=3, tiled=True)  94.1 us
    ppermute x11, waiting for transfers between devices, shifted(): lax.ppermute(value, axis, [(source, source + steps) for source in range(l...  81.8 us
    all_to_all x12, waiting for transfers between devices, sent_to_all(): lax.all_to_all(jnp.broadcast_to(array[None], (peers, *array.shape)), axis...  76.2 us
    all_gather x1, waiting for transfers between devices, from_root(): lax.all_gather(array, axis)  66 us
    another operation x1, loops' own time, shards(): arrived, stored = lax.fori_loop(0, step_count, advance, (initial, stored))  43.2 us
    all_to_all x12, starting transfers between devices, sent_to_all(): lax.all_to_all(jnp.broadcast_to(array[None], (peers, *array.shape)), axis...  41.7 us
  transfers between devices with their start and end apart: 25, of which 25 were waited for; matrix products, arithmetic and copies ran while one was open for 0% of the time, Pallas kernels for 0%

commit v1 on v0

v1 whole, which is shorter than its diff:
```python
import functools

import jax
import jax.numpy as jnp
from jax import lax
from jax.experimental import pallas as pl
from jax.experimental.pallas import tpu as pltpu
from jax.sharding import PartitionSpec as P

HEAD_DIM = 128
ADAPTER_RANK = 16
ADAPTER_JOBS = 4
LANES = 128
MESH = pl.DeviceIdType.MESH
F32 = jnp.float32
BF16 = jnp.bfloat16


def relay_kernel(
    dims,
    xin_ref,
    mask_ref,
    gain_ref,
    up_ref,
    down_hbm,
    wq_hbm,
    wk_hbm,
    wv_hbm,
    wo_hbm,
    out_ref,
    wcat,
    wout,
    upcat,
    xbuf,
    acc,
    rs_out,
    rs_in,
    ag_out,
    ebuf,
    xout,
    w_sem,
    d_send,
    d_recv,
    e_send,
    e_recv,
    ea_send,
    x_recv,
    ag_send,
    rs_send,
    rs_recv,
    o_send,
    o_recv,
):
    S, T, Q, M, C, W = dims
    s = lax.axis_index("section")
    t = lax.axis_index("tensor")
    D = C * T
    heads = C // HEAD_DIM
    per = S * T // T // (S // 2) * T
    lane = lax.broadcasted_iota(jnp.int32, (M, LANES), 1)

    def dev(sec, ten):
        return {"section": sec, "tensor": ten}

    def weight_copies():
        cps = [
            pltpu.make_async_copy(wq_hbm, wcat.at[:, pl.ds(0, C)], w_sem.at[0]),
            pltpu.make_async_copy(wk_hbm, wcat.at[:, pl.ds(C, C)], w_sem.at[1]),
            pltpu.make_async_copy(wv_hbm, wcat.at[:, pl.ds(2 * C, C)], w_sem.at[2]),
            pltpu.make_async_copy(
                down_hbm,
                wcat.at[pl.ds(pl.multiple_of(t * C, C), C), pl.ds(3 * C, LANES)],
                w_sem.at[3],
            ),
        ]
        for b in range(T):
            cps.append(
                pltpu.make_async_copy(wo_hbm.at[:, pl.ds(b * C, C)], wout.at[b], w_sem.at[4 + b])
            )
        return cps

    for cp in weight_copies():
        cp.start()

    barrier = pltpu.get_barrier_semaphore()

    def greet(i, c):
        sec = i // T
        ten = i % T

        @pl.when(jnp.logical_not(jnp.logical_and(sec == s, ten == t)))
        def _():
            pl.semaphore_signal(barrier, inc=1, device_id=dev(sec, ten), device_id_type=MESH)

        return c

    lax.fori_loop(0, S * T, greet, 0)
    pl.semaphore_wait(barrier, S * T - 1)

    home = s // 2
    slot = (s % 2) * T + t

    def entry_copy(q):
        return pltpu.make_async_remote_copy(
            src_ref=xin_ref.at[q],
            dst_ref=ebuf.at[slot],
            send_sem=e_send.at[q],
            recv_sem=e_recv.at[slot],
            device_id=dev(q, home),
            device_id_type=MESH,
        )

    def entry_start(q, c):
        mine = jnp.logical_and(q == s, t == home)

        @pl.when(jnp.logical_not(mine))
        def _():
            entry_copy(q).start()

        @pl.when(mine)
        def _():
            ebuf[slot] = xin_ref[q]

        return c

    lax.fori_loop(0, S, entry_start, 0)

    def down_copy(k):
        return pltpu.make_async_remote_copy(
            src_ref=down_hbm,
            dst_ref=wcat.at[pl.ds(pl.multiple_of(t * C, C), C), pl.ds(3 * C, LANES)],
            send_sem=d_send.at[k - 1],
            recv_sem=d_recv.at[k - 1],
            device_id=dev(s, lax.rem(t + k, T)),
            device_id_type=MESH,
        )

    for k in (2, 1, 3):
        down_copy(k).start()

    upcat[...] = jnp.zeros_like(upcat)
    upcat[0 : upcat.shape[0] // 2, 0:C] = up_ref[0]
    upcat[upcat.shape[0] // 2 :, C:] = up_ref[1]

    def entry_wait(i, c):
        src_s = 2 * t + i // T
        src_t = i % T

        @pl.when(jnp.logical_not(jnp.logical_and(src_s == s, src_t == t)))
        def _():
            pltpu.make_async_remote_copy(
                src_ref=xin_ref.at[0],
                dst_ref=ebuf.at[i],
                send_sem=e_send.at[0],
                recv_sem=e_recv.at[i],
                device_id=dev(s, t),
                device_id_type=MESH,
            ).wait_recv()

        return c

    pieces = 2 * T
    lax.fori_loop(0, pieces, entry_wait, 0)
    blocks = [jnp.zeros((M, LANES), F32) for _ in range(C // LANES)]
    for i in range(pieces):
        b, o = divmod(i * W, LANES)
        val = ebuf[i].astype(F32)
        val = jnp.where(lane < W, val, 0.0)
        if o:
            val = pltpu.roll(val, o, 1)
        if o + W <= LANES:
            blocks[b] = blocks[b] + val
        else:
            blocks[b] = blocks[b] + jnp.where(lane >= o, val, 0.0)
            blocks[b + 1] = blocks[b + 1] + jnp.where(lane < o + W - LANES, val, 0.0)
    entered = jnp.concatenate(blocks, axis=1).astype(BF16)

    def entry_spread(k):
        return pltpu.make_async_remote_copy(
            src_ref=ag_out.at[Q],
            dst_ref=xbuf.at[s, t],
            send_sem=ea_send.at[k],
            recv_sem=x_recv.at[s, t],
            device_id=dev(0, lax.rem(t + k, T)),
            device_id_type=MESH,
        )

    ag_out[Q] = entered
    for k in (2, 1, 3):
        entry_spread(k).start()

    @pl.when(s > 0)
    def _():
        entry_spread(0).start()

    @pl.when(s == 0)
    def _():
        xbuf[0, t] = entered

    for cp in weight_copies():
        cp.wait()
    for k in (1, 3, 2):
        down_copy(k).wait_recv()

    row = lax.broadcasted_iota(jnp.int32, (M, M), 0)
    col = lax.broadcasted_iota(jnp.int32, (M, M), 1)
    causal = row >= col

    def rs_copy(q, k):
        other = lax.rem(t + k, T)
        return pltpu.make_async_remote_copy(
            src_ref=rs_out.at[q, k],
            dst_ref=rs_in.at[q, k],
            send_sem=rs_send.at[q, k],
            recv_sem=rs_recv.at[q, k],
            device_id=dev(s, other),
            device_id_type=MESH,
        )

    def ag_copy(q, k):
        return pltpu.make_async_remote_copy(
            src_ref=ag_out.at[q],
            dst_ref=xbuf.at[q, t],
            send_sem=ag_send.at[q, k],
            recv_sem=x_recv.at[q, t],
            device_id=dev(s + 1, lax.rem(t + k, T)),
            device_id_type=MESH,
        )

    def exit_copy(q, i):
        return pltpu.make_async_remote_copy(
            src_ref=xout.at[q, i],
            dst_ref=out_ref.at[q],
            send_sem=o_send.at[q, i],
            recv_sem=o_recv.at[q],
            device_id=dev(2 * t + i // T, i % T),
            device_id_type=MESH,
        )

    def phase_a(q):
        ss = jnp.zeros((M, LANES), F32)
        for k in (0, 1, 3, 2):
            p = lax.rem(t + k, T)

            def arrive():
                pltpu.make_async_remote_copy(
                    src_ref=ag_out.at[0],
                    dst_ref=xbuf.at[q, p],
                    send_sem=ag_send.at[0, 0],
                    recv_sem=x_recv.at[q, p],
                    device_id=dev(s, t),
                    device_id_type=MESH,
                ).wait_recv()

            if k == 0:
                pl.when(jnp.logical_not(jnp.logical_and(s == 0, q == 0)))(arrive)
            else:
                arrive()
            xf = xbuf[q, p].astype(F32)
            sq = xf * xf
            for b in range(C // LANES):
                ss = ss + sq[:, b * LANES : (b + 1) * LANES]
            xg = (xf * gain_ref[p]).astype(BF16)
            prod = jnp.dot(
                xg, wcat[pl.ds(pl.multiple_of(p * C, C), C), :], preferred_element_type=F32
            )
            if k == 0:
                acc[...] = prod
            else:
                acc[...] += prod
        return ss

    def phase_b(q, ss):
        r = lax.rsqrt(jnp.sum(ss, axis=1, keepdims=True) * (1.0 / D) + 1e-05)
        codes = (acc[:, 3 * C :] * r * mask_ref[q]).astype(BF16)
        low = jnp.dot(codes, upcat[...], preferred_element_type=F32)
        mixed = []
        for h in range(heads):
            a, b = h * HEAD_DIM, (h + 1) * HEAD_DIM
            qh = (acc[:, a:b] * r + low[:, a:b]).astype(BF16)
            kh = (acc[:, C + a : C + b] * r).astype(BF16)
            vh = (acc[:, 2 * C + a : 2 * C + b] * r + low[:, C + a : C + b]).astype(BF16)
            sc = lax.dot_general(
                qh, kh, (((1,), (1,)), ((), ())), preferred_element_type=F32
            ) * (HEAD_DIM ** (-0.5))
            sc = jnp.where(causal, sc, -jnp.inf)
            top = jnp.max(sc, axis=1, keepdims=True)
            wts = jnp.exp(sc - top)
            prob = (wts / jnp.sum(wts, axis=1, keepdims=True)).astype(BF16)
            mixed.append(jnp.dot(prob, vh, preferred_element_type=F32).astype(BF16))
        mix = jnp.concatenate(mixed, axis=1)
        for k in (2, 1, 3, 0):
            other = lax.rem(t + k, T)
            part = jnp.dot(mix, wout[other], preferred_element_type=F32).astype(BF16)
            rs_out[q, k] = part
            if k:
                rs_copy(q, k).start()

    def phase_c(q):
        total = xbuf[q, t].astype(F32) + rs_out[q, 0].astype(F32)
        for k in (1, 3, 2):
            rs_copy(q, k).wait_recv()
        for k in (1, 3, 2):
            total = total + rs_in[q, k].astype(F32)

        @pl.when(s < S - 1)
        def _():
            ag_out[q] = total.astype(BF16)
            for k in (2, 1, 3, 0):
                ag_copy(q, k).start()

        @pl.when(s == S - 1)
        def _():
            ag_out[q] = total.astype(BF16)
            for i in range(pieces):
                b, o = divmod(i * W, LANES)
                val = total[:, b * LANES : (b + 1) * LANES]
                if o + W > LANES:
                    nxt = total[:, (b + 1) * LANES : (b + 2) * LANES]
                    val = jnp.where(lane >= o, val, nxt)
                if o:
                    val = pltpu.roll(val, LANES - o, 1)
                xout[q, i] = val.astype(BF16)

            for i in range(pieces - 1):
                exit_copy(q, i).start()

            @pl.when(t < T - 1)
            def _():
                exit_copy(q, pieces - 1).start()

            @pl.when(t == T - 1)
            def _():
                out_ref[q] = xout[q, pieces - 1]

    def step(q, c):
        ss = phase_a(q)
        phase_b(q, ss)
        phase_c(q)
        return c

    lax.fori_loop(0, Q, step, 0)

    last = jnp.logical_and(s == S - 1, t == T - 1)

    def finish(q, c):
        @pl.when(jnp.logical_not(last))
        def _():
            pltpu.make_async_remote_copy(
                src_ref=xout.at[q, 0],
                dst_ref=out_ref.at[q],
                send_sem=o_send.at[q, 0],
                recv_sem=o_recv.at[q],
                device_id=dev(s, t),
                device_id_type=MESH,
            ).wait_recv()

        for k in (1, 2, 3):
            rs_copy(q, k).wait_send()

        @pl.when(s < S - 1)
        def _():
            for k in range(T):
                ag_copy(q, k).wait_send()

        @pl.when(s == S - 1)
        def _():
            for i in range(pieces - 1):
                exit_copy(q, i).wait_send()

            @pl.when(t < T - 1)
            def _():
                exit_copy(q, pieces - 1).wait_send()

        @pl.when(jnp.logical_not(jnp.logical_and(q == s, t == home)))
        def _():
            entry_copy(q).wait_send()

        return c

    lax.fori_loop(0, Q, finish, 0)
    for k in (1, 2, 3):
        down_copy(k).wait_send()
        entry_spread(k).wait_send()

    @pl.when(s > 0)
    def _():
        entry_spread(0).wait_send()


def shards(
    inputs,
    sequence_jobs,
    entry_sequence,
    layer_norm_gain,
    frozen_query_matrix,
    frozen_key_matrix,
    frozen_value_matrix,
    frozen_output_matrix,
    adapter_down_maps,
    adapter_up_maps,
):
    S = lax.axis_size("section")
    T = lax.axis_size("tensor")
    batches, groups, M, W = inputs.shape
    Q = batches * groups
    C = frozen_query_matrix.shape[2]
    D = C * T
    ranks = adapter_down_maps.shape[2]
    ordered = jnp.take(inputs, entry_sequence, axis=0).reshape(Q, M, W)
    xin = jnp.pad(ordered, ((0, 0), (0, 0), (0, LANES - W)))
    jobs = jnp.take(sequence_jobs, entry_sequence, axis=0).reshape(Q)
    column_job = jnp.arange(ranks, dtype=jnp.int32) // ADAPTER_RANK % ADAPTER_JOBS
    mask = jnp.where(column_job[None, :] == jobs[:, None], 2.0, 0.0).astype(F32).reshape(Q, 1, ranks)
    gain = layer_norm_gain.reshape(T, 1, C)

    vm = pl.BlockSpec(memory_space=pltpu.VMEM)
    hb = pl.BlockSpec(memory_space=pl.ANY)
    dma = pltpu.SemaphoreType.DMA
    out = pl.pallas_call(
        functools.partial(relay_kernel, (S, T, Q, M, C, W)),
        out_shape=jax.ShapeDtypeStruct((Q, M, LANES), BF16),
        in_specs=[vm, vm, vm, vm, hb, hb, hb, hb, hb],
        out_specs=vm,
        scratch_shapes=[
            pltpu.VMEM((D, 3 * C + ranks), BF16),
            pltpu.VMEM((T, C, C), BF16),
            pltpu.VMEM((ranks, 2 * C), BF16),
            pltpu.VMEM((Q, T, M, C), BF16),
            pltpu.VMEM((M, 3 * C + ranks), F32),
            pltpu.VMEM((Q, T, M, C), BF16),
            pltpu.VMEM((Q, T, M, C), BF16),
            pltpu.VMEM((Q + 1, M, C), BF16),
            pltpu.VMEM((2 * T, M, LANES), BF16),
            pltpu.VMEM((Q, 2 * T, M, LANES), BF16),
            dma((4 + T,)),
            dma((3,)),
            dma((3,)),
            dma((S,)),
            dma((2 * T,)),
            dma((T,)),
            dma((Q, T)),
            dma((Q, T)),
            dma((Q, T)),
            dma((Q, T)),
            dma((Q, 2 * T)),
            dma((Q,)),
        ],
        compiler_params=pltpu.CompilerParams(
            collective_id=0, has_side_effects=True, vmem_limit_bytes=56 * 1024 * 1024
        ),
        name="relay",
    )(
        xin,
        mask,
        gain,
        adapter_up_maps[0],
        adapter_down_maps[0],
        frozen_query_matrix[0],
        frozen_key_matrix[0],
        frozen_value_matrix[0],
        frozen_output_matrix[0],
    )
    return out[:, :, :W].reshape(batches, groups, M, W)


def solution(mesh):
    in_specs = (
        P("dp", None, None, ("section", "tensor")),
        P("dp", None, None),
        P("dp"),
        P("section", None),
        P("section", None, "tensor"),
        P("section", None, "tensor"),
        P("section", None, "tensor"),
        P("section", "tensor", None),
        P("section", "tensor", None),
        P("section", None, None, "tensor"),
    )
    out_specs = P("dp", None, None, ("section", "tensor"))
    return jax.shard_map(shards, mesh=mesh, in_specs=in_specs, out_specs=out_specs, check_vma=False)
```

time: 948 us -> 228 us (0.24)
  waiting for transfers between devices: 318 us -> 0 us
  blocking collectives: 263 us -> 0 us
  Pallas kernels: 0 us -> 221 us
  starting transfers between devices: 177 us -> 0 us
  local copies, waits for them, and re-layouts: 59.7 us -> 4.4 us
  matrix products: 52.2 us -> 0 us
  loops' own time: 43.9 us -> 0 us
  between operations: 13.5 us -> 0.03 us
  other arithmetic: 14.4 us -> 2.13 us
    all_to_all x11 -> x0, blocking collectives: 263 us -> none  [sent_to_all(): lax.all_to_all(jnp.broadcast_to(array[None], (peers, *array.shape)), axis...]
    pallas_call x0 -> x1, Pallas kernels: none -> 221 us  [shards(): pl.pallas_call(functools.partial(relay_kernel, (S, T, Q, M, C, W)), out_s...]
    all_gather x2 -> x0, waiting for transfers between devices: 160 us -> none  [the longest x1 94.1 us: shards(): entire = lax.all_gather(inputs, ('section', 'tensor'), axis=3, tiled=True)]
    ppermute x11 -> x0, starting transfers between devices: 136 us -> none  [shifted(): lax.ppermute(value, axis, [(source, source + steps) for source in range(l...]
    ppermute x11 -> x0, waiting for transfers between devices: 81.8 us -> none  [shifted(): lax.ppermute(value, axis, [(source, source + steps) for source in range(l...]
    all_to_all x12 -> x0, waiting for transfers between devices: 76.2 us -> none  [sent_to_all(): lax.all_to_all(jnp.broadcast_to(array[None], (peers, *array.shape)), axis...]
    dot_general x36 -> x0, matrix products: 52.2 us -> none  [the longest x4 11.3 us: final_output(): jnp.dot(normalized_input, value_matrix, preferred_element_type=jnp.float32)]
    another operation x23 -> x0, loops' own time: 43.9 us -> none  [the longest x1 43.2 us: shards(): arrived, stored = lax.fori_loop(0, step_count, advance, (initial, stored))]
  transfers between devices with their start and end apart: 25 -> 0, of which waited for: 25 -> 0; matrix products, arithmetic and copies ran while one was open for 0% -> 0% of each run, Pallas kernels for 0% -> 0%
where the time goes in v1:
time: 228 us; the launch traced here: 227 us
  Pallas kernels  221 us (97%)
  local copies, waits for them, and re-layouts  4.4 us (2%)
    pallas_call x1, Pallas kernels, shards(): pl.pallas_call(functools.partial(relay_kernel, (S, T, Q, M, C, W)), out_s...  221 us

profile of v1, /device:TPU:1, one launch (start us, length us, event | category | flops | bytes accessed | tf_op | source)
XLA Modules:
  0.0 227.5 jit_solution(4682533908877726298)
XLA Ops:
  0.0 0.0 copy-start
  0.0 0.7 compare_and_fusion
  0.7 0.1 broadcast_in_dim.29
  0.8 0.1 broadcast_in_dim.30
  0.9 0.7 compare_select_fusion.1
  1.5 0.8 copy.12
  2.3 0.6 gather_fusion.1
  2.9 0.1 gather.15
  3.0 0.7 compare_select_fusion.mask_ref
  3.6 0.0 copy-done
  3.6 0.6 gather_fusion
  4.2 0.1 bitcast_select_fusion
  4.3 0.7 pad.4.xin_ref
  5.0 220.9 %relay.1 = bf16[8,64,128]{2,1,0:T(8,128)(2,1)} custom-call(bf16[8,64,128]{2,1,0:T(8,128)(2,1)} %pad.4.xin_ref, f32[8,1,128]{2,1,0:T(1,128)} %compare_select_fusion.mask_ref, f32[4,1,640]{2,1,0:T(1,128)} %bitcast.19, bf16[2,64,640]{2,1,0:T(8,128)(2,1)} %bitcast.17, bf16[640,128]{1,0:T(8,128)(2,1)} %bitcast.18, bf16[2560,640]{1,0:T(8,128)(2,1)} %bitcast.12, ...), custom_call_target="tpu_custom_call" | custom-call | tf_op jit(solution)/shard_map/relay/pallas_call | solution.py:420
  225.9 1.6 copy.14
  (3 shorter events, 0.0 us)
Async XLA Ops:
  0.0 3.6 %copy-start = (bf16[4,2,64,80]{3,2,1,0:T(8,128)(2,1)S(1)}, bf16[4,2,64,80]{3,2,1,0:T(8,128)(2,1)}, u32[]{:S(2)}) copy-start(bf16[4,2,64,80]{3,2,1,0:T(8,128)(2,1)} %param.10) | copy-start | bytes 245764

commit v2 on v1

--- a/solution.py
+++ b/solution.py
@@ -11,6 +11,7 @@
 ADAPTER_RANK = 16
 ADAPTER_JOBS = 4
 LANES = 128
+UNITS_PER_SEQUENCE = 2
 MESH = pl.DeviceIdType.MESH
 F32 = jnp.float32
 BF16 = jnp.bfloat16
@@ -18,8 +19,9 @@
 
 def relay_kernel(
     dims,
+    entry_ref,
+    jobs_ref,
     xin_ref,
-    mask_ref,
     gain_ref,
     up_ref,
     down_hbm,
@@ -31,11 +33,14 @@
     wcat,
     wout,
     upcat,
+    kbuf,
+    vbuf,
     xbuf,
     acc,
     rs_out,
     rs_in,
     ag_out,
+    estage,
     ebuf,
     xout,
     w_sem,
@@ -51,13 +56,16 @@
     o_send,
     o_recv,
 ):
-    S, T, Q, M, C, W = dims
+    S, T, Q, L, H, C, W = dims
+    M = L // H
+    U = Q * H
+    groups = xin_ref.shape[1]
     s = lax.axis_index("section")
     t = lax.axis_index("tensor")
     D = C * T
     heads = C // HEAD_DIM
-    per = S * T // T // (S // 2) * T
     lane = lax.broadcasted_iota(jnp.int32, (M, LANES), 1)
+    long_lane = lax.broadcasted_iota(jnp.int32, (L, LANES), 1)
 
     def dev(sec, ten):
         return {"section": sec, "tensor": ten}
@@ -95,6 +103,15 @@
         return c
 
     lax.fori_loop(0, S * T, greet, 0)
+
+    estage[...] = jnp.zeros_like(estage)
+    for q in range(Q):
+        estage[q, :, 0:W] = xin_ref[entry_ref[q // groups], q % groups]
+    kbuf[...] = jnp.zeros_like(kbuf)
+    vbuf[...] = jnp.zeros_like(vbuf)
+    upcat[...] = jnp.zeros_like(upcat)
+    upcat[0 : upcat.shape[0] // 2, 0:C] = up_ref[0]
+    upcat[upcat.shape[0] // 2 :, C:] = up_ref[1]
     pl.semaphore_wait(barrier, S * T - 1)
 
     home = s // 2
@@ -102,7 +119,7 @@
 
     def entry_copy(q):
         return pltpu.make_async_remote_copy(
-            src_ref=xin_ref.at[q],
+            src_ref=estage.at[q],
             dst_ref=ebuf.at[slot],
             send_sem=e_send.at[q],
             recv_sem=e_recv.at[slot],
@@ -119,7 +136,7 @@
 
         @pl.when(mine)
         def _():
-            ebuf[slot] = xin_ref[q]
+            ebuf[slot] = estage[q]
 
         return c
 
@@ -135,12 +152,10 @@
             device_id_type=MESH,
         )
 
-    for k in (2, 1, 3):
-        down_copy(k).start()
-
-    upcat[...] = jnp.zeros_like(upcat)
-    upcat[0 : upcat.shape[0] // 2, 0:C] = up_ref[0]
-    upcat[upcat.shape[0] // 2 :, C:] = up_ref[1]
+    @pl.when(s == 0)
+    def _():
+        for k in (2, 1, 3):
+            down_copy(k).start()
 
     def entry_wait(i, c):
         src_s = 2 * t + i // T
@@ -149,7 +164,7 @@
         @pl.when(jnp.logical_not(jnp.logical_and(src_s == s, src_t == t)))
         def _():
             pltpu.make_async_remote_copy(
-                src_ref=xin_ref.at[0],
+                src_ref=estage.at[0],
                 dst_ref=ebuf.at[i],
                 send_sem=e_send.at[0],
                 recv_sem=e_recv.at[i],
@@ -161,50 +176,56 @@
 
     pieces = 2 * T
     lax.fori_loop(0, pieces, entry_wait, 0)
-    blocks = [jnp.zeros((M, LANES), F32) for _ in range(C // LANES)]
+    blocks = [jnp.zeros((L, LANES), F32) for _ in range(C // LANES)]
     for i in range(pieces):
         b, o = divmod(i * W, LANES)
         val = ebuf[i].astype(F32)
-        val = jnp.where(lane < W, val, 0.0)
+        val = jnp.where(long_lane < W, val, 0.0)
         if o:
             val = pltpu.roll(val, o, 1)
         if o + W <= LANES:
             blocks[b] = blocks[b] + val
         else:
-            blocks[b] = blocks[b] + jnp.where(lane >= o, val, 0.0)
-            blocks[b + 1] = blocks[b + 1] + jnp.where(lane < o + W - LANES, val, 0.0)
+            blocks[b] = blocks[b] + jnp.where(long_lane >= o, val, 0.0)
+            blocks[b + 1] = blocks[b + 1] + jnp.where(long_lane < o + W - LANES, val, 0.0)
     entered = jnp.concatenate(blocks, axis=1).astype(BF16)
 
-    def entry_spread(k):
+    def entry_spread(h, k):
         return pltpu.make_async_remote_copy(
-            src_ref=ag_out.at[Q],
-            dst_ref=xbuf.at[s, t],
-            send_sem=ea_send.at[k],
-            recv_sem=x_recv.at[s, t],
+            src_ref=ag_out.at[U + h],
+            dst_ref=xbuf.at[H * s + h, t],
+            send_sem=ea_send.at[h, k],
+            recv_sem=x_recv.at[H * s + h, t],
             device_id=dev(0, lax.rem(t + k, T)),
             device_id_type=MESH,
         )
 
-    ag_out[Q] = entered
-    for k in (2, 1, 3):
-        entry_spread(k).start()
+    for h in range(H):
+        ag_out[U + h] = entered[h * M : (h + 1) * M]
+        for k in (2, 1, 3):
+            entry_spread(h, k).start()
+
+        @pl.when(s > 0)
+        def _():
+            entry_spread(h, 0).start()
+
+        @pl.when(s == 0)
+        def _():
+            xbuf[h, t] = entered[h * M : (h + 1) * M]
 
     @pl.when(s > 0)
     def _():
-        entry_spread(0).start()
-
-    @pl.when(s == 0)
-    def _():
-        xbuf[0, t] = entered
+        for k in (2, 1, 3):
+            down_copy(k).start()
 
     for cp in weight_copies():
         cp.wait()
     for k in (1, 3, 2):
         down_copy(k).wait_recv()
 
-    row = lax.broadcasted_iota(jnp.int32, (M, M), 0)
-    col = lax.broadcasted_iota(jnp.int32, (M, M), 1)
-    causal = row >= col
+    row = lax.broadcasted_iota(jnp.int32, (M, L), 0)
+    col = lax.broadcasted_iota(jnp.int32, (M, L), 1)
+    owner = lax.broadcasted_iota(jnp.int32, (1, LANES), 1) // ADAPTER_RANK % ADAPTER_JOBS
 
     def rs_copy(q, k):
         other = lax.rem(t + k, T)
@@ -253,7 +274,7 @@
                 ).wait_recv()
 
             if k == 0:
-                pl.when(jnp.logical_not(jnp.logical_and(s == 0, q == 0)))(arrive)
+                pl.when(jnp.logical_not(jnp.logical_and(s == 0, q < H)))(arrive)
             else:
                 arrive()
             xf = xbuf[q, p].astype(F32)
@@ -272,14 +293,21 @@
 
     def phase_b(q, ss):
         r = lax.rsqrt(jnp.sum(ss, axis=1, keepdims=True) * (1.0 / D) + 1e-05)
-        codes = (acc[:, 3 * C :] * r * mask_ref[q]).astype(BF16)
+        seq = q // H
+        part = q % H
+        job = jobs_ref[seq % groups, entry_ref[seq // groups]]
+        codes = jnp.where(owner == job, acc[:, 3 * C :] * (r * 2.0), 0.0).astype(BF16)
         low = jnp.dot(codes, upcat[...], preferred_element_type=F32)
+        here = pl.ds(pl.multiple_of(part * M, M), M)
+        kbuf[here, :] = (acc[:, C : 2 * C] * r).astype(BF16)
+        vbuf[here, :] = (acc[:, 2 * C : 3 * C] * r + low[:, C:]).astype(BF16)
+        causal = row + part * M >= col
         mixed = []
         for h in range(heads):
             a, b = h * HEAD_DIM, (h + 1) * HEAD_DIM
             qh = (acc[:, a:b] * r + low[:, a:b]).astype(BF16)
-            kh = (acc[:, C + a : C + b] * r).astype(BF16)
-            vh = (acc[:, 2 * C + a : 2 * C + b] * r + low[:, C + a : C + b]).astype(BF16)
+            kh = kbuf[:, a:b]
+            vh = vbuf[:, a:b]
             sc = lax.dot_general(
                 qh, kh, (((1,), (1,)), ((), ())), preferred_element_type=F32
             ) * (HEAD_DIM ** (-0.5))
@@ -291,8 +319,7 @@
         mix = jnp.concatenate(mixed, axis=1)
         for k in (2, 1, 3, 0):
             other = lax.rem(t + k, T)
-            part = jnp.dot(mix, wout[other], preferred_element_type=F32).astype(BF16)
-            rs_out[q, k] = part
+            rs_out[q, k] = jnp.dot(mix, wout[other], preferred_element_type=F32).astype(BF16)
             if k:
                 rs_copy(q, k).start()
 
@@ -334,12 +361,18 @@
                 out_ref[q] = xout[q, pieces - 1]
 
     def step(q, c):
-        ss = phase_a(q)
-        phase_b(q, ss)
-        phase_c(q)
+        @pl.when(q < U)
+        def _():
+            ss = phase_a(q)
+            phase_b(q, ss)
+
+        @pl.when(q > 0)
+        def _():
+            phase_c(q - 1)
+
         return c
 
-    lax.fori_loop(0, Q, step, 0)
+    lax.fori_loop(0, U + 1, step, 0)
 
     last = jnp.logical_and(s == S - 1, t == T - 1)
 
@@ -372,20 +405,24 @@
             def _():
                 exit_copy(q, pieces - 1).wait_send()
 
-        @pl.when(jnp.logical_not(jnp.logical_and(q == s, t == home)))
+        return c
+
+    lax.fori_loop(0, U, finish, 0)
+    for q in range(S):
+
+        @pl.when(jnp.logical_not(jnp.logical_and(s == q, t == home)))
         def _():
             entry_copy(q).wait_send()
 
-        return c
-
-    lax.fori_loop(0, Q, finish, 0)
     for k in (1, 2, 3):
         down_copy(k).wait_send()
-        entry_spread(k).wait_send()
+        for h in range(H):
+            entry_spread(h, k).wait_send()
 
     @pl.when(s > 0)
     def _():
-        entry_spread(0).wait_send()
+        for h in range(H):
+            entry_spread(h, 0).wait_send()
 
 
 def shards(
@@ -402,57 +439,60 @@
 ):
     S = lax.axis_size("section")
     T = lax.axis_size("tensor")
-    batches, groups, M, W = inputs.shape
+    batches, groups, L, W = inputs.shape
     Q = batches * groups
+    H = UNITS_PER_SEQUENCE
+    U, M = Q * H, L // H
     C = frozen_query_matrix.shape[2]
     D = C * T
     ranks = adapter_down_maps.shape[2]
-    ordered = jnp.take(inputs, entry_sequence, axis=0).reshape(Q, M, W)
-    xin = jnp.pad(ordered, ((0, 0), (0, 0), (0, LANES - W)))
-    jobs = jnp.take(sequence_jobs, entry_sequence, axis=0).reshape(Q)
-    column_job = jnp.arange(ranks, dtype=jnp.int32) // ADAPTER_RANK % ADAPTER_JOBS
-    mask = jnp.where(column_job[None, :] == jobs[:, None], 2.0, 0.0).astype(F32).reshape(Q, 1, ranks)
+    jobs = jnp.transpose(sequence_jobs, (1, 2, 0)).reshape(groups, batches)
     gain = layer_norm_gain.reshape(T, 1, C)
 
     vm = pl.BlockSpec(memory_space=pltpu.VMEM)
     hb = pl.BlockSpec(memory_space=pl.ANY)
+    sm = pl.BlockSpec(memory_space=pltpu.SMEM)
     dma = pltpu.SemaphoreType.DMA
     out = pl.pallas_call(
-        functools.partial(relay_kernel, (S, T, Q, M, C, W)),
-        out_shape=jax.ShapeDtypeStruct((Q, M, LANES), BF16),
-        in_specs=[vm, vm, vm, vm, hb, hb, hb, hb, hb],
+        functools.partial(relay_kernel, (S, T, Q, L, H, C, W)),
+        out_shape=jax.ShapeDtypeStruct((U, M, LANES), BF16),
+        in_specs=[sm, sm, vm, vm, vm, hb, hb, hb, hb, hb],
         out_specs=vm,
         scratch_shapes=[
             pltpu.VMEM((D, 3 * C + ranks), BF16),
             pltpu.VMEM((T, C, C), BF16),
             pltpu.VMEM((ranks, 2 * C), BF16),
-            pltpu.VMEM((Q, T, M, C), BF16),
+            pltpu.VMEM((L, C), BF16),
+            pltpu.VMEM((L, C), BF16),
+            pltpu.VMEM((U, T, M, C), BF16),
             pltpu.VMEM((M, 3 * C + ranks), F32),
-            pltpu.VMEM((Q, T, M, C), BF16),
-            pltpu.VMEM((Q, T, M, C), BF16),
-            pltpu.VMEM((Q + 1, M, C), BF16),
-            pltpu.VMEM((2 * T, M, LANES), BF16),
-            pltpu.VMEM((Q, 2 * T, M, LANES), BF16),
+            pltpu.VMEM((U, T, M, C), BF16),
+            pltpu.VMEM((U, T, M, C), BF16),
+            pltpu.VMEM((U + H, M, C), BF16),
+            pltpu.VMEM((Q, L, LANES), BF16),
+            pltpu.VMEM((2 * T, L, LANES), BF16),
+            pltpu.VMEM((U, 2 * T, M, LANES), BF16),
             dma((4 + T,)),
             dma((3,)),
             dma((3,)),
             dma((S,)),
             dma((2 * T,)),
-            dma((T,)),
-            dma((Q, T)),
-            dma((Q, T)),
-            dma((Q, T)),
-            dma((Q, T)),
-            dma((Q, 2 * T)),
-            dma((Q,)),
+            dma((H, T)),
+            dma((U, T)),
+            dma((U, T)),
+            dma((U, T)),
+            dma((U, T)),
+            dma((U, 2 * T)),
+            dma((U,)),
         ],
         compiler_params=pltpu.CompilerParams(
             collective_id=0, has_side_effects=True, vmem_limit_bytes=56 * 1024 * 1024
         ),
         name="relay",
     )(
-        xin,
-        mask,
+        entry_sequence,
+        jobs,
+        inputs,
         gain,
         adapter_up_maps[0],
         adapter_down_maps[0],
@@ -461,7 +501,7 @@
         frozen_value_matrix[0],
         frozen_output_matrix[0],
     )
-    return out[:, :, :W].reshape(batches, groups, M, W)
+    return out[:, :, :W].reshape(batches, groups, L, W)
 
 
 def solution(mesh):

time: 228 us -> 204 us (0.89)
  Pallas kernels: 221 us -> 203 us
  local copies, waits for them, and re-layouts: 4.4 us -> 1.57 us
    pallas_call x1, Pallas kernels: 221 us -> 203 us  [shards(): pl.pallas_call(functools.partial(relay_kernel, (S, T, Q, L, H, C, W)), ou...]
where the time goes in v2:
time: 204 us
  Pallas kernels  203 us (100%)
    pallas_call x1, Pallas kernels, shards(): pl.pallas_call(functools.partial(relay_kernel, (S, T, Q, L, H, C, W)), ou...  203 us

profile of v2, /device:TPU:1, one launch (start us, length us, event | category | flops | bytes accessed | tf_op | source)
XLA Modules:
  0.0 204.4 jit_solution(8917706388640177204)
XLA Ops:
  0.0 202.8 %relay.1 = bf16[16,32,128]{2,1,0:T(8,128)(2,1)} custom-call(s32[4]{0:T(128)} %entry_ref.1, s32[2,4]{1,0:T(2,128)} %bitcast.20, bf16[4,2,64,80]{3,2,1,0:T(8,128)(2,1)} %xin_ref.1, f32[4,1,640]{2,1,0:T(1,128)} %bitcast.19, bf16[2,64,640]{2,1,0:T(8,128)(2,1)} %bitcast.17, bf16[640,128]{1,0:T(8,128)(2,1)} %bitcast.18, bf16[2560,640]{1,0:T(8,128)(2,1)} %bitcast.12, ...), custom_call_target="tpu_custom_call" | custom-call | tf_op jit(solution)/shard_map/relay/pallas_call | solution.py:456
  202.8 1.6 copy.12

commit v3 on v2

--- a/solution.py
+++ b/solution.py
@@ -72,12 +72,12 @@
 
     def weight_copies():
         cps = [
-            pltpu.make_async_copy(wq_hbm, wcat.at[:, pl.ds(0, C)], w_sem.at[0]),
-            pltpu.make_async_copy(wk_hbm, wcat.at[:, pl.ds(C, C)], w_sem.at[1]),
-            pltpu.make_async_copy(wv_hbm, wcat.at[:, pl.ds(2 * C, C)], w_sem.at[2]),
+            pltpu.make_async_copy(wq_hbm, wcat.at[:, pl.ds(LANES, C)], w_sem.at[0]),
+            pltpu.make_async_copy(wk_hbm, wcat.at[:, pl.ds(LANES + C, C)], w_sem.at[1]),
+            pltpu.make_async_copy(wv_hbm, wcat.at[:, pl.ds(LANES + 2 * C, C)], w_sem.at[2]),
             pltpu.make_async_copy(
                 down_hbm,
-                wcat.at[pl.ds(pl.multiple_of(t * C, C), C), pl.ds(3 * C, LANES)],
+                wcat.at[pl.ds(pl.multiple_of(t * C, C), C), pl.ds(0, LANES)],
                 w_sem.at[3],
             ),
         ]
@@ -145,7 +145,7 @@
     def down_copy(k):
         return pltpu.make_async_remote_copy(
             src_ref=down_hbm,
-            dst_ref=wcat.at[pl.ds(pl.multiple_of(t * C, C), C), pl.ds(3 * C, LANES)],
+            dst_ref=wcat.at[pl.ds(pl.multiple_of(t * C, C), C), pl.ds(0, LANES)],
             send_sem=d_send.at[k - 1],
             recv_sem=d_recv.at[k - 1],
             device_id=dev(s, lax.rem(t + k, T)),
@@ -258,25 +258,20 @@
             device_id_type=MESH,
         )
 
-    def phase_a(q):
-        ss = jnp.zeros((M, LANES), F32)
-        for k in (0, 1, 3, 2):
+    def arrive(q, p):
+        pltpu.make_async_remote_copy(
+            src_ref=ag_out.at[0],
+            dst_ref=xbuf.at[q, p],
+            send_sem=ag_send.at[0, 0],
+            recv_sem=x_recv.at[q, p],
+            device_id=dev(s, t),
+            device_id_type=MESH,
+        ).wait_recv()
+
+    def product(q, ks, ss):
+        total = None
+        for k in ks:
             p = lax.rem(t + k, T)
-
-            def arrive():
-                pltpu.make_async_remote_copy(
-                    src_ref=ag_out.at[0],
-                    dst_ref=xbuf.at[q, p],
-                    send_sem=ag_send.at[0, 0],
-                    recv_sem=x_recv.at[q, p],
-                    device_id=dev(s, t),
-                    device_id_type=MESH,
-                ).wait_recv()
-
-            if k == 0:
-                pl.when(jnp.logical_not(jnp.logical_and(s == 0, q < H)))(arrive)
-            else:
-                arrive()
             xf = xbuf[q, p].astype(F32)
             sq = xf * xf
             for b in range(C // LANES):
@@ -285,10 +280,17 @@
             prod = jnp.dot(
                 xg, wcat[pl.ds(pl.multiple_of(p * C, C), C), :], preferred_element_type=F32
             )
-            if k == 0:
-                acc[...] = prod
-            else:
-                acc[...] += prod
+            total = prod if total is None else total + prod
+        return total, ss
+
+    def phase_a(q):
+        pl.when(jnp.logical_not(jnp.logical_and(s == 0, q < H)))(lambda: arrive(q, t))
+        for k in (1, 3):
+            arrive(q, lax.rem(t + k, T))
+        acc[...], ss = product(q, (0, 1, 3), jnp.zeros((M, LANES), F32))
+        arrive(q, lax.rem(t + 2, T))
+        last, ss = product(q, (2,), ss)
+        acc[...] += last
         return ss
 
     def phase_b(q, ss):
@@ -296,32 +298,30 @@
         seq = q // H
         part = q % H
         job = jobs_ref[seq % groups, entry_ref[seq // groups]]
-        codes = jnp.where(owner == job, acc[:, 3 * C :] * (r * 2.0), 0.0).astype(BF16)
+        codes = jnp.where(owner == job, acc[:, :LANES] * (r * 2.0), 0.0).astype(BF16)
         low = jnp.dot(codes, upcat[...], preferred_element_type=F32)
         here = pl.ds(pl.multiple_of(part * M, M), M)
-        kbuf[here, :] = (acc[:, C : 2 * C] * r).astype(BF16)
-        vbuf[here, :] = (acc[:, 2 * C : 3 * C] * r + low[:, C:]).astype(BF16)
+        q0, k0, v0 = LANES, LANES + C, LANES + 2 * C
+        kbuf[here, :] = (acc[:, k0:v0] * r).astype(BF16)
+        vbuf[here, :] = (acc[:, v0 : v0 + C] * r + low[:, C:]).astype(BF16)
         causal = row + part * M >= col
         mixed = []
         for h in range(heads):
             a, b = h * HEAD_DIM, (h + 1) * HEAD_DIM
-            qh = (acc[:, a:b] * r + low[:, a:b]).astype(BF16)
-            kh = kbuf[:, a:b]
-            vh = vbuf[:, a:b]
+            qh = (acc[:, q0 + a : q0 + b] * r + low[:, a:b]).astype(BF16)
             sc = lax.dot_general(
-                qh, kh, (((1,), (1,)), ((), ())), preferred_element_type=F32
+                qh, kbuf[:, a:b], (((1,), (1,)), ((), ())), preferred_element_type=F32
             ) * (HEAD_DIM ** (-0.5))
             sc = jnp.where(causal, sc, -jnp.inf)
-            top = jnp.max(sc, axis=1, keepdims=True)
-            wts = jnp.exp(sc - top)
-            prob = (wts / jnp.sum(wts, axis=1, keepdims=True)).astype(BF16)
-            mixed.append(jnp.dot(prob, vh, preferred_element_type=F32).astype(BF16))
+            wts = jnp.exp(sc - jnp.max(sc, axis=1, keepdims=True))
+            mean = jnp.dot(wts.astype(BF16), vbuf[:, a:b], preferred_element_type=F32)
+            mixed.append((mean / jnp.sum(wts, axis=1, keepdims=True)).astype(BF16))
         mix = jnp.concatenate(mixed, axis=1)
         for k in (2, 1, 3, 0):
             other = lax.rem(t + k, T)
             rs_out[q, k] = jnp.dot(mix, wout[other], preferred_element_type=F32).astype(BF16)
-            if k:
-                rs_copy(q, k).start()
+        for k in (2, 1, 3):
+            rs_copy(q, k).start()
 
     def phase_c(q):
         total = xbuf[q, t].astype(F32) + rs_out[q, 0].astype(F32)

time: 204 us -> 202 us (level)
  no operation moved by 1% of the time
where the time goes in v3:
time: 202 us
  Pallas kernels  201 us (100%)
    pallas_call x1, Pallas kernels, shards(): pl.pallas_call(functools.partial(relay_kernel, (S, T, Q, L, H, C, W)), ou...  201 us

profile of v3, /device:TPU:1, one launch (start us, length us, event | category | flops | bytes accessed | tf_op | source)
XLA Modules:
  0.0 202.4 jit_solution(5266397167024730187)
XLA Ops:
  0.0 200.8 %relay.1 = bf16[16,32,128]{2,1,0:T(8,128)(2,1)} custom-call(s32[4]{0:T(128)} %entry_ref.1, s32[2,4]{1,0:T(2,128)} %bitcast.20, bf16[4,2,64,80]{3,2,1,0:T(8,128)(2,1)} %xin_ref.1, f32[4,1,640]{2,1,0:T(1,128)} %bitcast.19, bf16[2,64,640]{2,1,0:T(8,128)(2,1)} %bitcast.17, bf16[640,128]{1,0:T(8,128)(2,1)} %bitcast.18, bf16[2560,640]{1,0:T(8,128)(2,1)} %bitcast.12, ...), custom_call_target="tpu_custom_call" | custom-call | tf_op jit(solution)/shard_map/relay/pallas_call | solution.py:456
  200.8 1.6 copy.12

commit v4 on v3

--- a/solution.py
+++ b/solution.py
@@ -288,34 +288,40 @@
         for k in (1, 3):
             arrive(q, lax.rem(t + k, T))
         acc[...], ss = product(q, (0, 1, 3), jnp.zeros((M, LANES), F32))
-        arrive(q, lax.rem(t + 2, T))
-        last, ss = product(q, (2,), ss)
-        acc[...] += last
-        return ss
-
-    def phase_b(q, ss):
+        far = lax.rem(t + 2, T)
+        arrive(q, far)
+        xf = xbuf[q, far].astype(F32)
+        sq = xf * xf
+        for b in range(C // LANES):
+            ss = ss + sq[:, b * LANES : (b + 1) * LANES]
+        return ss, (xf * gain_ref[far]).astype(BF16), pl.ds(pl.multiple_of(far * C, C), C)
+
+    def phase_b(q, ss, xg, rows):
+        code_sum = acc[:, :LANES] + jnp.dot(
+            xg, wcat[rows, 0:LANES], preferred_element_type=F32
+        )
         r = lax.rsqrt(jnp.sum(ss, axis=1, keepdims=True) * (1.0 / D) + 1e-05)
         seq = q // H
         part = q % H
         job = jobs_ref[seq % groups, entry_ref[seq // groups]]
-        codes = jnp.where(owner == job, acc[:, :LANES] * (r * 2.0), 0.0).astype(BF16)
+        codes = jnp.where(owner == job, code_sum * (r * 2.0), 0.0).astype(BF16)
         low = jnp.dot(codes, upcat[...], preferred_element_type=F32)
         here = pl.ds(pl.multiple_of(part * M, M), M)
-        q0, k0, v0 = LANES, LANES + C, LANES + 2 * C
-        kbuf[here, :] = (acc[:, k0:v0] * r).astype(BF16)
-        vbuf[here, :] = (acc[:, v0 : v0 + C] * r + low[:, C:]).astype(BF16)
+        full = acc[:, LANES:] + jnp.dot(xg, wcat[rows, LANES:], preferred_element_type=F32)
+        kbuf[here, :] = (full[:, C : 2 * C] * r).astype(BF16)
+        vbuf[here, :] = (full[:, 2 * C :] * r + low[:, C:]).astype(BF16)
         causal = row + part * M >= col
         mixed = []
         for h in range(heads):
             a, b = h * HEAD_DIM, (h + 1) * HEAD_DIM
-            qh = (acc[:, q0 + a : q0 + b] * r + low[:, a:b]).astype(BF16)
+            qh = (full[:, a:b] * r + low[:, a:b]).astype(BF16)
             sc = lax.dot_general(
                 qh, kbuf[:, a:b], (((1,), (1,)), ((), ())), preferred_element_type=F32
             ) * (HEAD_DIM ** (-0.5))
             sc = jnp.where(causal, sc, -jnp.inf)
             wts = jnp.exp(sc - jnp.max(sc, axis=1, keepdims=True))
             mean = jnp.dot(wts.astype(BF16), vbuf[:, a:b], preferred_element_type=F32)
-            mixed.append((mean / jnp.sum(wts, axis=1, keepdims=True)).astype(BF16))
+            mixed.append((mean * (1.0 / jnp.sum(wts, axis=1, keepdims=True))).astype(BF16))
         mix = jnp.concatenate(mixed, axis=1)
         for k in (2, 1, 3, 0):
             other = lax.rem(t + k, T)
@@ -363,8 +369,7 @@
     def step(q, c):
         @pl.when(q < U)
         def _():
-            ss = phase_a(q)
-            phase_b(q, ss)
+            phase_b(q, *phase_a(q))
 
         @pl.when(q > 0)
         def _():

time: 202 us -> 207 us (1.025)
  Pallas kernels: 201 us -> 206 us
    pallas_call x1, Pallas kernels: 201 us -> 206 us  [shards(): pl.pallas_call(functools.partial(relay_kernel, (S, T, Q, L, H, C, W)), ou...]
where the time goes in v4:
time: 207 us
  Pallas kernels  206 us (100%)
    pallas_call x1, Pallas kernels, shards(): pl.pallas_call(functools.partial(relay_kernel, (S, T, Q, L, H, C, W)), ou...  206 us

profile of v4, /device:TPU:1, one launch (start us, length us, event | category | flops | bytes accessed | tf_op | source)
XLA Modules:
  0.0 207.1 jit_solution(13402376512799602271)
XLA Ops:
  0.0 205.5 %relay.1 = bf16[16,32,128]{2,1,0:T(8,128)(2,1)} custom-call(s32[4]{0:T(128)} %entry_ref.1, s32[2,4]{1,0:T(2,128)} %bitcast.20, bf16[4,2,64,80]{3,2,1,0:T(8,128)(2,1)} %xin_ref.1, f32[4,1,640]{2,1,0:T(1,128)} %bitcast.19, bf16[2,64,640]{2,1,0:T(8,128)(2,1)} %bitcast.17, bf16[640,128]{1,0:T(8,128)(2,1)} %bitcast.18, bf16[2560,640]{1,0:T(8,128)(2,1)} %bitcast.12, ...), custom_call_target="tpu_custom_call" | custom-call | tf_op jit(solution)/shard_map/relay/pallas_call | solution.py:461
  205.5 1.6 copy.12
